TPU v7x, 1024 devices: a whole 8x8x8 slice. The times are simulated.
1024 devices in a mesh: node: 32 (over z_lo, y, core), rep: 32 (over x, z_hi).
Axes of the slice: x: 8, y: 8, z: 8 (z_hi: 4, z_lo: 2; z = z_hi * 2 + z_lo), core: 2. Of those that a mesh axis runs over, the one named last changes fastest.
Arguments:
- tokens: bfloat16 [262144, 2048], P(('node', 'rep')), may hold values from -60 to 60
- cotangent: bfloat16 [262144, 512], P(('node', 'rep')), may hold values from -6 to 6
- value_weight: bfloat16 [2048, 512], P('node'), may hold values from -0.25 to 0.25
Outputs:
- input_grad: bfloat16 [262144, 2048], P(('node', 'rep'))
- update: float32 [2048, 512], P('node')
All inputs are finite; a program needn't handle non-finite values.
Results may differ from a plain program's by a relative error of at most 0.025.
Values may be sent and summed in bfloat16 or wider, within the bound.
A program may use at most 32 MiB of HBM per device.

v0:
```python
import math

import jax
import jax.numpy as jnp
from jax import lax
from jax.sharding import PartitionSpec as P

DIN = 2048
HD = 128
NS_ITERS = 5


coef_a = 3.4445
coef_b = -4.775
coef_c = 2.0315
epsilon = 1e-07


def in_blocks(shard, dim, length):
    dims = shard.shape
    pieces = shard.reshape(*dims[:dim], length, dims[dim] // length, *dims[dim + 1 :])
    return jnp.moveaxis(pieces, dim, 0)


def summed_on_arrival(shard, axis, dim):
    pieces = in_blocks(shard, dim, lax.axis_size(axis))
    arrived = lax.all_to_all(pieces, axis, split_axis=0, concat_axis=0, tiled=True)
    return arrived.astype(jnp.float32).sum(axis=0)


def gathered_total(shard, axis):
    return lax.all_gather(shard, axis).sum(0)


def per_device(tokens, cotangent, value_weight):
    width = value_weight.shape[1]
    local_rows = value_weight.shape[0]
    heads = width // HD
    input_grad = lax.dot_general(
        cotangent,
        lax.all_gather(value_weight, "node", axis=0, tiled=True),
        (((1,), (1,)), ((), ())),
        preferred_element_type=jnp.float32,
    ).astype(jnp.bfloat16)
    partial_rows = summed_on_arrival(
        lax.dot_general(
            tokens, cotangent, (((0,), (0,)), ((), ())), preferred_element_type=jnp.float32
        ).astype(jnp.bfloat16),
        "node",
        0,
    )
    gradient = gathered_total(partial_rows, "rep")
    blocks = gradient.reshape(local_rows, heads, HD)
    local_raw = jnp.einsum("rhi,rhj->hij", blocks, blocks, precision=lax.Precision.HIGHEST)
    gram_raw = gathered_total(local_raw, "node")
    squares = jnp.einsum("hii->h", gram_raw)
    divisor = jnp.sqrt(squares) + epsilon
    start_iterate = blocks / divisor[None, :, None]
    gram = gram_raw / (divisor * divisor)[:, None, None]
    identity = jnp.broadcast_to(jnp.eye(HD, dtype=jnp.float32), (heads, HD, HD))
    total = identity
    for step in range(NS_ITERS):
        factor = (
            coef_a * identity
            + coef_b * gram
            + coef_c * jnp.einsum("hij,hjk->hik", gram, gram, precision=lax.Precision.HIGHEST)
        )
        total = jnp.einsum("hij,hjk->hik", total, factor, precision=lax.Precision.HIGHEST)
        if step + 1 < NS_ITERS:
            halfway = jnp.einsum("hij,hjk->hik", gram, factor, precision=lax.Precision.HIGHEST)
            gram = jnp.einsum("hji,hjk->hik", factor, halfway, precision=lax.Precision.HIGHEST)
    iterate = jnp.einsum("rhi,hij->rhj", start_iterate, total, precision=lax.Precision.HIGHEST)
    update = 0.2 * math.sqrt(DIN) * iterate.reshape(local_rows, width)
    return (input_grad, update)


def solution(mesh):
    in_specs = (P(("node", "rep"), None), P(("node", "rep"), None), P("node", None))
    out_specs = (P(("node", "rep"), None), P("node", None))
    return jax.shard_map(
        per_device, mesh=mesh, in_specs=in_specs, out_specs=out_specs, check_vma=False
    )
```

profile of v0, /device:TPU:1, one launch (start us, length us, event | category | flops | bytes accessed | tf_op | source)
XLA Modules:
  0.0 357.5 jit_solution(11234164317037267739)
XLA Ops:
  7.2 1.2 copy-done
  8.4 1.7 convolution_convert_fusion
  10.1 65.7 %all_to_all.5 = bf16[32,64,512]{2,1,0:T(8,128)(2,1)S(1)} all-to-all(bf16[32,64,512]{2,1,0:T(8,128)(2,1)S(1)} %bitcast.53), channel_id=1, replica_groups=mesh['node'=32,'rep'=32] {'node'}, dimensions={0} | all-to-all | bytes 4194304 | tf_op jit(solution)/shard_map/all_to_all | solution.py:27
  75.8 0.9 convert_reduce_fusion
  76.9 0.7 all-gather.6.cloned.1.call-update
  77.6 110.3 %all-gather.8.cloned.1.call-done = f32[2048,512]{1,0:T(8,128)} async-done(((f32[64,512]{1,0:T(8,128)}), f32[2048,512]{1,0:T(8,128)}) %all-gather.8.cloned.1.call-update) | async-done | bytes 4194320 | tf_op jit(solution)/shard_map/all_gather | solution.py:32
  187.9 2.6 reduce_sum.37
  190.5 1.3 fusion.6
  191.9 65.7 %all-gather.6.cloned.1.call-done = bf16[2048,512]{1,0:T(8,128)(2,1)} async-done(((bf16[64,512]{1,0:T(8,128)(2,1)}), bf16[2048,512]{1,0:T(8,128)(2,1)}) %all-gather.6.cloned.1.call-update) | async-done | bytes 2097168 | tf_op jit(solution)/shard_map/all_gather | solution.py:41
  257.6 3.3 convolution_convert_fusion.1
  260.9 76.9 %all-gather.10.cloned.1.call-done = f32[128,128,128]{2,1,0:T(8,128)} async-done(((f32[4,128,128]{2,1,0:T(8,128)}), f32[128,128,128]{2,1,0:T(8,128)}) %all-gather.10.cloned.1.call-update) | async-done | bytes 8388624 | tf_op jit(solution)/shard_map/all_gather | solution.py:32
  337.8 3.8 %reduce_sum.38 = f32[4,128,128]{2,1,0:T(8,128)S(1)} reduce(f32[32,4,128,128]{3,2,1,0:T(8,128)} %bitcast.54, f32[]{:T(128)} %constant.1.clone.1), dimensions={0}, to_apply=%region_2.0 | reduce | flops 2031616 | bytes 8650756 | tf_op jit(solution)/shard_map/reduce_sum | solution.py:32
  341.8 0.5 fusion.4
  342.3 0.4 fusion.14
  342.7 0.6 fusion.16
  343.3 0.4 fusion.3
  343.7 0.4 fusion.18
  344.1 0.6 fusion.19
  344.7 0.4 fusion.2
  345.1 0.4 fusion.21
  345.5 0.6 fusion.22
  346.1 0.4 fusion.1
  346.5 0.4 fusion.24
  346.9 0.6 fusion.25
  347.5 0.4 fusion
  347.9 0.4 fusion.10
  348.3 0.4 fusion.17
  348.7 0.4 fusion.20
  349.1 0.4 fusion.23
  349.5 0.4 fusion.26
  350.0 0.3 fusion.5
  350.3 0.7 copy.46
  (15 shorter events, 0.5 us)
Async XLA Ops:
  7.2 1.2 copy-start
  7.2 180.7 %all-gather.8.cloned.1.call-start = ((), (), s32[]{:S(2)}) async-start(), calls=%async_computation.2 | async-start | bytes 4325376 | tf_op jit(solution)/shard_map/all_gather | solution.py:32
  76.8 180.8 %all-gather.6.cloned.1.call-start = ((), (), s32[]{:S(2)}) async-start(), calls=%async_computation.1 | async-start | bytes 2162688 | tf_op jit(solution)/shard_map/all_gather | solution.py:41
  77.6 260.3 %all-gather.10.cloned.1.call-start = ((), (), s32[]{:S(2)}) async-start(), calls=%async_computation.3 | async-start | bytes 8650752 | tf_op jit(solution)/shard_map/all_gather | solution.py:32
  187.9 69.7 %copy-start.1 = (bf16[256,512]{1,0:T(8,128)(2,1)S(1)}, bf16[256,512]{1,0:T(8,128)(2,1)}, u32[]{:S(2)}) copy-start(bf16[256,512]{1,0:T(8,128)(2,1)} %param.4) | copy-start | bytes 786436
Sparse Core Ops, SparseCore 0:
  76.9 110.9 all-gather.7
  190.6 66.9 all-gather.5
  260.3 77.4 all-gather.9
where the time goes:
time: 358 us
  waiting for transfers between devices  254 us (71%)
  blocking collectives  65.7 us (18%)
  matrix products  14.6 us (4%)
  between operations  13.9 us (4%)
  other arithmetic  7.61 us (2%)
    all_gather x2, waiting for transfers between devices, gathered_total(): return lax.all_gather(shard, axis).sum(0)  187 us
    all_to_all x1, blocking collectives, summed_on_arrival(): lax.all_to_all(pieces, axis, split_axis=0, concat_axis=0, tiled=True)  65.7 us
    all_gather x1, waiting for transfers between devices, per_device(): lax.all_gather(value_weight, 'node', axis=0, tiled=True)  65.7 us
  transfers between devices with their start and end apart: 3, of which 3 were waited for; matrix products, arithmetic and copies ran while one was open for 2% of the time, Pallas kernels for 0%

commit v1 on v0

v1 whole, which is shorter than its diff:
```python
import functools
import math

import jax
import jax.numpy as jnp
from jax import lax
from jax.experimental import pallas as pl
from jax.experimental.pallas import tpu as pltpu
from jax.sharding import PartitionSpec as P

MESH = pl.DeviceIdType.MESH

DIN = 2048
HD = 128
NS_ITERS = 5

coef_a = 3.4445
coef_b = -4.775
coef_c = 2.0315
epsilon = 1e-07

NX, NY, NZ, NZH = 8, 8, 8, 4
FAR = (4, 3, 5, 2, 6, 1, 7)


def mm(a, b):
    return jnp.dot(a, b, precision=lax.Precision.HIGHEST, preferred_element_type=jnp.float32)


def kernel(
    tok_hbm, cot_hbm, w_hbm, ig_hbm, up_ref,
    tok, cot, wfull, ig,
    term, other, px, py, rx, ry, sx, sy, r2x, r2y,
    qz, rz, gh, af, rc, bslice, rg, gram, ub,
    load_sem, out_sem, d2d_s, d2d_r, w1_s, w1_r, w2_s, w2_r, w3_s, w3_r,
    x1_s, x1_r, y1_s, y1_r, x2_s, x2_r, y2_s, y2_r, z_s, z_r, g_s, g_r,
    c_s, c_r, b_s, b_r, a_s, a_r, u_s, u_r,
):
    node, rep = lax.axis_index("node"), lax.axis_index("rep")
    core = lax.rem(node, 2)
    y = lax.rem(lax.div(node, 2), NY)
    zl = lax.div(node, 2 * NY)
    x, zh = lax.div(rep, NZH), lax.rem(rep, NZH)
    z = zh * 2 + zl

    def dev(x_=None, y_=None, z_=None, core_=None):
        x_ = x if x_ is None else x_
        y_ = y if y_ is None else y_
        z_ = z if z_ is None else z_
        core_ = core if core_ is None else core_
        zl_, zh_ = lax.rem(z_, 2), lax.div(z_, 2)
        return {"node": (zl_ * NY + y_) * 2 + core_, "rep": x_ * NZH + zh_}

    def ahead(at, d, n):
        return lax.rem(at + d, n)

    def send(src, dst, ssem, rsem, to):
        copy = pltpu.make_async_remote_copy(
            src_ref=src, dst_ref=dst, send_sem=ssem, recv_sem=rsem, device_id=to, device_id_type=MESH
        )
        copy.start()
        return copy

    z_pair = z + 1 - 2 * zl
    partner = dev(core_=1 - core)

    barrier = pltpu.get_barrier_semaphore()
    peers = [dev(x_=ahead(x, d, NX)) for d in FAR]
    peers += [dev(y_=ahead(y, d, NY)) for d in FAR]
    peers += [dev(z_=ahead(z, d, NZ)) for d in FAR]
    peers += [partner, dev(z_=z_pair, core_=1 - core)]
    for to in peers:
        pl.semaphore_signal(barrier, inc=1, device_id=to, device_id_type=MESH)

    load_cot = pltpu.make_async_copy(cot_hbm, cot, load_sem.at[0])
    load_cot.start()
    loads = []
    for k in range(8):
        columns = pl.ds((k % 2) * 1024 + (k // 2) * 256, 256)
        load = pltpu.make_async_copy(tok_hbm.at[:, columns], tok.at[:, columns], load_sem.at[2 + k])
        load.start()
        loads.append(load)
    load_w = pltpu.make_async_copy(w_hbm.at[zh], wfull.at[zl, y, core, zh], load_sem.at[1])
    load_w.start()

    unsent = []
    load_cot.wait()
    d2d = []
    for k in range(4):
        halves = []
        for lo in range(2):
            loads[2 * k + lo].wait()
            t = lax.dot_general(
                tok[:, lo * 1024 + k * 256 : lo * 1024 + k * 256 + 256],
                cot[...],
                (((0,), (0,)), ((), ())),
                preferred_element_type=jnp.float32,
            )
            halves.append(t.reshape(2, 2, 8, 8, 512))
        term[2 * k : 2 * k + 2] = jnp.concatenate(halves, axis=3).astype(jnp.bfloat16)
        if k == 0:
            pl.semaphore_wait(barrier, len(peers))
        d2d.append(
            send(term.at[pl.ds(2 * k, 2), 1 - core], other.at[pl.ds(2 * k, 2)], d2d_s.at[k], d2d_r.at[k], partner)
        )
    unsent += d2d

    load_w.wait()
    w1 = []
    for i, d in enumerate(FAR):
        mine = wfull.at[zl, y, core, zh]
        w1.append(send(mine, mine, w1_s.at[i], w1_r.at[i], dev(y_=ahead(y, d, NY))))
    unsent += w1

    for k in range(4):
        d2d[k].wait_recv()
        for b in (2 * k, 2 * k + 1):
            s = term[b, core].astype(jnp.float32) + other[b].astype(jnp.float32)
            s = s.astype(jnp.bfloat16)
            px[:, b] = s[:, :, :256]
            py[b] = s[:, :, 256:]

    first = []
    for i, d in enumerate(FAR):
        to_x, to_y = ahead(x, d, NX), ahead(y, d, NY)
        first.append(send(px.at[to_x], rx.at[i], x1_s.at[i], x1_r.at[i], dev(x_=to_x)))
        first.append(send(py.at[to_y], ry.at[i], y1_s.at[i], y1_r.at[i], dev(y_=to_y)))
    unsent += first

    for copy in w1:
        copy.wait_recv()
    w2 = []
    for i, d in enumerate(FAR):
        mine = wfull.at[zl, :, core, zh]
        w2.append(send(mine, mine, w2_s.at[i], w2_r.at[i], dev(z_=ahead(z, d, NZ))))
    unsent += w2

    for copy in first:
        copy.wait_recv()
    for b in range(8):
        total_x = px[x, b].astype(jnp.float32)
        total_y = py[y, b].astype(jnp.float32)
        for i in range(7):
            total_x += rx[i, b].astype(jnp.float32)
            total_y += ry[i, b].astype(jnp.float32)
        sx[b] = total_x.astype(jnp.bfloat16)
        sy[b] = total_y.astype(jnp.bfloat16)

    second = []
    for i, d in enumerate(FAR):
        to_x, to_y = ahead(x, d, NX), ahead(y, d, NY)
        second.append(send(sx.at[to_y], r2x.at[i], y2_s.at[i], y2_r.at[i], dev(y_=to_y)))
        second.append(send(sy.at[to_x], r2y.at[i], x2_s.at[i], x2_r.at[i], dev(x_=to_x)))
    unsent += second
    for copy in second:
        copy.wait_recv()
    total_x = sx[y].astype(jnp.float32)
    total_y = sy[x].astype(jnp.float32)
    for i in range(7):
        total_x += r2x[i].astype(jnp.float32)
        total_y += r2y[i].astype(jnp.float32)
    for lo in range(2):
        for h in range(4):
            source = total_x if h < 2 else total_y
            qz[lo, h] = source[8 * lo : 8 * lo + 8, (h % 2) * HD : (h % 2) * HD + HD]

    third = []
    for i, d in enumerate(FAR):
        to_z = ahead(z, d, NZ)
        third.append(
            send(qz.at[lax.rem(to_z, 2), lax.div(to_z, 2)], rz.at[i], z_s.at[i], z_r.at[i], dev(z_=to_z))
        )
    unsent += third
    for copy in third:
        copy.wait_recv()
    rows = qz[zl, zh]
    for i in range(7):
        rows += rz[i]
    gh[x] = rows

    gather = []
    for i, d in enumerate(FAR):
        gather.append(send(gh.at[x], gh.at[x], g_s.at[i], g_r.at[i], dev(x_=ahead(x, d, NX))))
    unsent += gather
    for copy in gather:
        copy.wait_recv()

    g = gh[...].reshape(64, HD)
    partial = lax.dot_general(
        g, g, (((0,), (0,)), ((), ())), precision=lax.Precision.HIGHEST, preferred_element_type=jnp.float32
    )
    af[...] = partial.reshape(8, 16, HD)

    quad = [
        send(af.at[x], rc.at[0], c_s.at[0], c_r.at[0], partner),
        send(af.at[x], rc.at[1], c_s.at[1], c_r.at[1], dev(z_=z_pair)),
        send(af.at[x], rc.at[2], c_s.at[2], c_r.at[2], dev(z_=z_pair, core_=1 - core)),
    ]
    unsent += quad
    for copy in quad:
        copy.wait_recv()
    bslice[...] = af[x] + rc[0] + rc[1] + rc[2]

    over_y = []
    for i, d in enumerate(FAR):
        over_y.append(send(bslice, rg.at[i], b_s.at[i], b_r.at[i], dev(y_=ahead(y, d, NY))))
    unsent += over_y

    for copy in w2:
        copy.wait_recv()
    w3 = send(wfull.at[:, :, core], wfull.at[:, :, core], w3_s, w3_r, partner)
    unsent.append(w3)

    for copy in over_y:
        copy.wait_recv()
    total = bslice[...]
    for i in range(7):
        total += rg[i]
    gram[x] = total

    over_x = []
    for i, d in enumerate(FAR):
        over_x.append(send(gram.at[x], gram.at[x], a_s.at[i], a_r.at[i], dev(x_=ahead(x, d, NX))))
    unsent += over_x

    w3.wait_recv()
    outs = []
    for k in range(8):
        lo, b = k // 4, 2 * (k % 4)
        weight = wfull[lo, b : b + 2].reshape(256, 512)
        ig[:, k * 256 : k * 256 + 256] = lax.dot_general(
            cot[...], weight, (((1,), (1,)), ((), ())), preferred_element_type=jnp.float32
        ).astype(jnp.bfloat16)
        columns = pl.ds(k * 256, 256)
        out = pltpu.make_async_copy(ig.at[:, columns], ig_hbm.at[:, columns], out_sem.at[k])
        out.start()
        outs.append(out)

    for copy in over_x:
        copy.wait_recv()
    a = gram[...].reshape(HD, HD)
    row = lax.broadcasted_iota(jnp.int32, (HD, HD), 0)
    col = lax.broadcasted_iota(jnp.int32, (HD, HD), 1)
    eye = row == col
    identity = jnp.where(eye, 1.0, 0.0).astype(jnp.float32)
    square = jnp.sum(jnp.where(eye, a, 0.0), axis=0, keepdims=True)
    square = jnp.sum(square, axis=1, keepdims=True)
    divisor = jnp.sqrt(square) + epsilon
    a = a / (divisor * divisor)
    total = None
    for step in range(NS_ITERS):
        factor = coef_a * identity + coef_b * a + coef_c * mm(a, a)
        total = factor if total is None else mm(total, factor)
        if step + 1 < NS_ITERS:
            a = mm(factor, mm(a, factor))
    ub[zh] = (0.2 * math.sqrt(DIN)) * mm(gh[...].reshape(64, HD) / divisor, total)

    last = []
    for d in (1, 2, 3):
        to_z = lax.rem(zh + d, NZH) * 2 + zl
        last.append(send(ub.at[zh], ub.at[zh], u_s.at[d - 1], u_r.at[d - 1], dev(z_=to_z)))
    unsent += last
    for copy in last:
        copy.wait_recv()
    for h in range(4):
        up_ref[:, h * HD : h * HD + HD] = ub[h]

    for copy in unsent:
        copy.wait_send()
    for out in outs:
        out.wait()


def per_device(tokens, cotangent, value_weight):
    bf16, f32 = jnp.bfloat16, jnp.float32
    vmem, dma = pltpu.VMEM, pltpu.SemaphoreType.DMA
    seven = [dma((7,)), dma((7,))]
    return pl.pallas_call(
        kernel,
        out_shape=(
            jax.ShapeDtypeStruct((256, DIN), bf16),
            jax.ShapeDtypeStruct((64, 512), f32),
        ),
        in_specs=[pl.BlockSpec(memory_space=pl.ANY)] * 3,
        out_specs=(pl.BlockSpec(memory_space=pl.ANY), pl.BlockSpec(memory_space=pltpu.VMEM)),
        scratch_shapes=[
            vmem((256, DIN), bf16),
            vmem((256, 512), bf16),
            vmem((2, NY, 2, NZH, 16, 512), bf16),
            vmem((256, DIN), bf16),
            vmem((8, 2, 8, 16, 512), bf16),
            vmem((8, 8, 16, 512), bf16),
            vmem((8, 8, 16, 256), bf16),
            vmem((8, 8, 16, 256), bf16),
            vmem((7, 8, 16, 256), bf16),
            vmem((7, 8, 16, 256), bf16),
            vmem((8, 16, 256), bf16),
            vmem((8, 16, 256), bf16),
            vmem((7, 16, 256), bf16),
            vmem((7, 16, 256), bf16),
            vmem((2, 4, 8, HD), f32),
            vmem((7, 8, HD), f32),
            vmem((8, 8, HD), f32),
            vmem((8, 16, HD), f32),
            vmem((3, 16, HD), f32),
            vmem((16, HD), f32),
            vmem((7, 16, HD), f32),
            vmem((8, 16, HD), f32),
            vmem((4, 64, HD), f32),
            dma((10,)), dma((8,)), dma((4,)), dma((4,)),
            *seven, *seven, dma, dma,
            *seven, *seven, *seven, *seven, *seven, *seven,
            dma((3,)), dma((3,)), *seven, *seven, dma((3,)), dma((3,)),
        ],
        compiler_params=pltpu.CompilerParams(
            collective_id=0, has_side_effects=True, vmem_limit_bytes=60 * 1024 * 1024
        ),
        name="whole",
    )(tokens, cotangent, value_weight.reshape(NZH, 16, 512))


def solution(mesh):
    in_specs = (P(("node", "rep"), None), P(("node", "rep"), None), P("node", None))
    out_specs = (P(("node", "rep"), None), P("node", None))
    return jax.shard_map(
        per_device, mesh=mesh, in_specs=in_specs, out_specs=out_specs, check_vma=False
    )
```

time: 358 us -> 85.8 us (0.24)
  the two profiles are of different devices: /device:TPU:1 before, /device:TPU:4 now
where the time goes in v1:
time: 85.8 us; the launch traced here: 85.6 us
  Pallas kernels  81.9 us (95%)
  local copies, waits for them, and re-layouts  3 us (3%)
    pallas_call x1, Pallas kernels, per_device(): pl.pallas_call(kernel, out_shape=(jax.ShapeDtypeStruct((256, DIN), bf16),...  81.9 us
    unnamed x4, local copies, waits for them, and re-layouts  3 us

profile of v1, /device:TPU:4, one launch (start us, length us, event | category | flops | bytes accessed | tf_op | source)
XLA Modules:
  0.0 85.6 jit_solution(12047227083892131326)
XLA Ops:
  0.6 81.9 %whole.1 = (bf16[256,2048]{1,0:T(8,128)(2,1)}, f32[64,512]{1,0:T(8,128)}) custom-call(bf16[256,2048]{1,0:T(8,128)(2,1)} %tok_hbm.1, bf16[256,512]{1,0:T(8,128)(2,1)} %cot_hbm.1, bf16[4,16,512]{2,1,0:T(8,128)(2,1)} %bitcast.1), custom_call_target="tpu_custom_call" | custom-call | tf_op jit(solution)/shard_map/whole/pallas_call | solution.py:278
  82.6 0.0 copy-start
  82.6 2.3 %copy.7 = bf16[256,2048]{1,0:T(8,128)(2,1)} copy(bf16[256,2048]{1,0:T(8,128)(2,1)} %get-tuple-element.4) | data formatting | bytes 2097152
  84.9 0.0 copy-done
  84.9 0.7 copy.8
Async XLA Ops:
  82.6 2.4 %copy-start = (f32[64,512]{1,0:T(8,128)S(1)}, f32[64,512]{1,0:T(8,128)}, u32[]{:S(2)}) copy-start(f32[64,512]{1,0:T(8,128)} %get-tuple-element.5) | copy-start | bytes 393220

commit v2 on v0

v2 whole, which is shorter than its diff:
```python
import functools
import math

import jax
import jax.numpy as jnp
from jax import lax
from jax.experimental import pallas as pl
from jax.experimental.pallas import tpu as pltpu
from jax.sharding import PartitionSpec as P

MESH = pl.DeviceIdType.MESH

DIN = 2048
HD = 128
NS_ITERS = 5

coef_a = 3.4445
coef_b = -4.775
coef_c = 2.0315
epsilon = 1e-07

NX, NY, NZ, NZH = 8, 8, 8, 4
FAR = (4, 3, 5, 2, 6, 1, 7)
EARLY, LATE = (3, 5, 2, 6), (4, 1, 7)
UPDATE_DTYPE = jnp.bfloat16
VMEM_LIMIT = 24 * 1024 * 1024


def mm(a, b):
    return jnp.dot(a, b, precision=lax.Precision.HIGHEST, preferred_element_type=jnp.float32)


def kernel(
    tok_hbm, cot_hbm, w_hbm, ig_ref, up_ref,
    tok, cot, wfull, wown,
    term, other, px, py, rx, ry, sx, sy, r2x, r2y,
    qz, rz, gh, af, rc, bslice, rg, gram, ub, uz,
    load_sem, d2d_s, d2d_r, w0_s, w0_r, w1_s, w1_r, w2_s, w2_r, w3_s, w3_r,
    x1_s, x1_r, y1_s, y1_r, x2_s, x2_r, y2_s, y2_r, z_s, z_r, g_s, g_r,
    c_s, c_r, b_s, b_r, a_s, a_r, u_s, v_s, u_r, go_sem,
):
    node, rep = lax.axis_index("node"), lax.axis_index("rep")
    core = lax.rem(node, 2)
    y = lax.rem(lax.div(node, 2), NY)
    zl = lax.div(node, 2 * NY)
    x, zh = lax.div(rep, NZH), lax.rem(rep, NZH)
    z = zh * 2 + zl

    def dev(x_=None, y_=None, z_=None, core_=None):
        to = {}
        if y_ is not None or z_ is not None or core_ is not None:
            low = zl if z_ is None else lax.rem(z_, 2)
            to["node"] = (low * NY + (y if y_ is None else y_)) * 2 + (core if core_ is None else core_)
        if x_ is not None or z_ is not None:
            to["rep"] = (x if x_ is None else x_) * NZH + (zh if z_ is None else lax.div(z_, 2))
        return to

    def ahead(at, d, n):
        return lax.rem(at + d, n)

    def describe(src, dst, ssem, rsem, to):
        return pltpu.make_async_remote_copy(
            src_ref=src, dst_ref=dst, send_sem=ssem, recv_sem=rsem, device_id=to, device_id_type=MESH
        )

    def send(src, dst, ssem, rsem, to):
        describe(src, dst, ssem, rsem, to).start()

    def wait(like, sem):
        pltpu.make_async_copy(like, like, sem).wait()

    partner = dev(core_=1 - core)

    load_cot = pltpu.make_async_copy(cot_hbm, cot, load_sem.at[0])
    load_cot.start()
    for k in range(4):
        for lo in range(2):
            columns = pl.ds(lo * 1024 + k * 256, 256)
            pltpu.make_async_copy(tok_hbm.at[:, columns], tok.at[:, columns], load_sem.at[2 + k]).start()
    load_w = pltpu.make_async_copy(w_hbm.at[zh], wown, load_sem.at[1])
    load_w.start()

    barrier = pltpu.get_barrier_semaphore()

    def greet(to):
        pl.semaphore_signal(barrier, inc=1, device_id=to, device_id_type=MESH)

    def z_hi_peer(d, core_):
        return dev(z_=lax.rem(zh + d, NZH) * 2 + zl, core_=core_)

    for d in FAR:
        greet(dev(z_=ahead(z, d, NZ)))

    @pl.when(core == 0)
    def _():
        for d in (2, 1, 3):
            greet(z_hi_peer(d, 1))

    for d in FAR:
        greet(dev(y_=ahead(y, d, NY)))

    @pl.when(core == 1)
    def _():
        for d in FAR:
            greet(dev(x_=ahead(x, d, NX)))

    greet(partner)

    def compute(k):
        wait(tok.at[:, pl.ds(0, 512)], load_sem.at[2 + k])
        for lo in range(2):
            t = lax.dot_general(
                tok[:, lo * 1024 + k * 256 : lo * 1024 + k * 256 + 256],
                cot[...],
                (((0,), (0,)), ((), ())),
                preferred_element_type=jnp.float32,
            )
            term[2 * k : 2 * k + 2, lo] = t.reshape(2, 8, 16, 512).astype(jnp.bfloat16)

    def piece(at):
        return wfull.at[lax.rem(at, 2), :, :, lax.div(at, 2)]

    def finish():
        for k in range(8):
            lo, b = k // 4, 2 * (k % 4)
            weight = wfull[lo, b : b + 2].reshape(256, 512)
            ig_ref[:, k * 256 : k * 256 + 256] = lax.dot_general(
                cot[...], weight, (((1,), (1,)), ((), ())), preferred_element_type=jnp.float32
            ).astype(jnp.bfloat16)

    def place():
        for h in range(4):
            up_ref[:, h * HD : h * HD + HD] = ub[h].astype(jnp.float32)

    to_partner = describe(wown, wfull.at[zl, y, 1, zh], w0_s, w0_r, partner)

    @pl.when(core == 0)
    def _():
        load_cot.wait()
        for k in range(4):
            compute(k)
            if k == 0:
                pl.semaphore_wait(barrier, 15)
            ys = pl.ds(2 * k, 2)
            send(term.at[ys], other.at[ys], d2d_s, d2d_r.at[k], partner)
            if k == 0:
                load_w.wait()
                wfull[zl, y, 0, zh] = wown[...]
            if k == 2:
                to_partner.wait_recv()
                mine = wfull.at[zl, y, :, zh]
                for d in FAR:
                    send(mine, mine, w1_s, w1_r, dev(y_=ahead(y, d, NY)))

        sevenths = wfull.at[0, pl.ds(0, 7), :, 0]
        four, three = wfull.at[0], wfull.at[0, :, :, pl.ds(0, 3)]
        wait(sevenths, w1_r)
        for d in EARLY:
            send(piece(z), piece(z), w2_s.at[0], w2_r.at[0], dev(z_=ahead(z, d, NZ)))
        send(piece(z), piece(z), w3_s, w3_r, partner)
        wait(four, w2_r.at[0])
        for d in EARLY:
            at = piece(lax.rem(z + NZ - d, NZ))
            send(at, at, w3_s, w3_r, partner)
        pl.semaphore_wait(go_sem, 1)
        for d in LATE:
            send(piece(z), piece(z), w2_s.at[1], w2_r.at[1], dev(z_=ahead(z, d, NZ)))
        wait(three, w2_r.at[1])
        for d in LATE:
            at = piece(lax.rem(z + NZ - d, NZ))
            send(at, at, w3_s, w3_r, partner)
        finish()
        wait(term, d2d_s)
        wait(sevenths, w1_s)
        wait(four, w2_s.at[0])
        wait(three, w2_s.at[1])
        wait(wfull, w3_s)
        wait(ub, u_r)
        place()

    @pl.when(core == 1)
    def _():
        load_cot.wait()
        compute(0)
        load_w.wait()
        pl.semaphore_wait(barrier, 25)
        to_partner.start()
        for k in range(1, 4):
            compute(k)

        for k in range(4):
            ys = pl.ds(2 * k, 2)
            wait(other.at[ys], d2d_r.at[k])
            for b in (2 * k, 2 * k + 1):
                for lo in range(2):
                    s = term[b, lo] + other[b, lo]
                    px[:, b, lo] = s[:, :, :256]
                    py[b, lo] = s[:, :, 256:]
            for b in (2 * k, 2 * k + 1):

                @pl.when(y != b)
                def _(b=b):
                    slot = lax.rem(b + NY - y, NY) - 1
                    send(py.at[b], ry.at[slot], y1_s, y1_r, dev(y_=b))

            if k % 2 == 1:
                ys = pl.ds(2 * k - 2, 4)
                for d in FAR:
                    to_x = ahead(x, d, NX)
                    send(px.at[to_x, ys], rx.at[d - 1, ys], x1_s, x1_r, dev(x_=to_x))

        wait(rx, x1_r)
        wait(ry, y1_r)
        for b in range(8):
            for lo in range(2):
                total_x = px[x, b, lo].astype(jnp.float32)
                total_y = py[y, lo, b].astype(jnp.float32)
                for i in range(7):
                    total_x += rx[i, b, lo].astype(jnp.float32)
                    total_y += ry[i, lo, b].astype(jnp.float32)
                sx[b, lo] = total_x.astype(jnp.bfloat16)
                sy[b, lo] = total_y.astype(jnp.bfloat16)

        for d in FAR:
            to_x, to_y = ahead(x, d, NX), ahead(y, d, NY)
            send(sx.at[to_y], r2x.at[d - 1], y2_s, y2_r, dev(y_=to_y))
            send(sy.at[to_x], r2y.at[d - 1], x2_s, x2_r, dev(x_=to_x))
        wait(r2x, y2_r)
        wait(r2y, x2_r)
        total_x = sx[y].astype(jnp.float32)
        total_y = sy[x].astype(jnp.float32)
        for i in range(7):
            total_x += r2x[i].astype(jnp.float32)
            total_y += r2y[i].astype(jnp.float32)
        for h in range(4):
            source = total_x if h < 2 else total_y
            qz[:, h] = source[:, :, (h % 2) * HD : (h % 2) * HD + HD]

        for d in FAR:
            to_z = ahead(z, d, NZ)
            send(qz.at[lax.rem(to_z, 2), lax.div(to_z, 2)], rz.at[d - 1], z_s, z_r, dev(z_=to_z))
        wait(rz, z_r)
        rows = qz[zl, zh]
        for i in range(7):
            rows += rz[i]
        gh[x] = rows

        for d in FAR:
            send(gh.at[x], gh.at[x], g_s, g_r, dev(x_=ahead(x, d, NX)))
        others = gh.at[pl.ds(0, 7)]
        wait(others, g_r)

        g = gh[...].reshape(128, HD)
        partial = lax.dot_general(
            g, g, (((0,), (0,)), ((), ())), precision=lax.Precision.HIGHEST, preferred_element_type=jnp.float32
        )
        af[...] = partial.reshape(8, 16, HD)

        send(af.at[x], rc, c_s, c_r, dev(z_=z + 1 - 2 * zl))
        wait(rc, c_r)
        pl.semaphore_signal(go_sem, inc=1, device_id=partner, device_id_type=MESH)
        bslice[...] = af[x] + rc[...]

        for d in FAR:
            send(bslice, rg.at[d - 1], b_s, b_r, dev(y_=ahead(y, d, NY)))
        wait(rg, b_r)
        total = bslice[...]
        for i in range(7):
            total += rg[i]
        gram[x] = total

        for d in FAR:
            send(gram.at[x], gram.at[x], a_s, a_r, dev(x_=ahead(x, d, NX)))
        wait(others, a_r)

        a = gram[...].reshape(HD, HD)
        row = lax.broadcasted_iota(jnp.int32, (HD, HD), 0)
        col = lax.broadcasted_iota(jnp.int32, (HD, HD), 1)
        eye = row == col
        identity = jnp.where(eye, 1.0, 0.0).astype(jnp.float32)
        square = jnp.sum(jnp.where(eye, a, 0.0), axis=0, keepdims=True)
        square = jnp.sum(square, axis=1, keepdims=True)
        divisor = jnp.sqrt(square) + epsilon
        a = a / (divisor * divisor)
        total = None
        for step in range(NS_ITERS):
            factor = coef_a * identity + coef_b * a + coef_c * mm(a, a)
            total = factor if total is None else mm(total, factor)
            if step + 1 < NS_ITERS:
                a = mm(factor, mm(a, factor))
        result = (0.2 * math.sqrt(DIN)) * mm(gh[...].reshape(128, HD) / divisor, total)
        result = result.astype(uz.dtype).reshape(2, 64, HD)
        uz[...] = result
        ub[zh] = result[1]

        for d in (2, 1, 3):
            send(uz.at[1], ub.at[zh], u_s, u_r, z_hi_peer(d, 1))
            send(uz.at[0], ub.at[zh], v_s, u_r, z_hi_peer(d, 0))
        send(uz.at[0], ub.at[zh], v_s, u_r, partner)

        wait(wfull, w3_r)
        finish()
        to_partner.wait_send()
        for like, sem in (
            (rx, x1_s), (ry, y1_s), (r2x, y2_s), (r2y, x2_s), (rz, z_s),
            (others, g_s), (rc, c_s), (rg, b_s), (others, a_s),
        ):
            wait(like, sem)
        three = ub.at[pl.ds(0, 3)]
        wait(three, u_r)
        place()
        wait(three, u_s)
        wait(ub, v_s)


def per_device(tokens, cotangent, value_weight):
    bf16, f32 = jnp.bfloat16, jnp.float32
    vmem, dma = pltpu.VMEM, pltpu.SemaphoreType.DMA
    args = tokens, cotangent, value_weight.reshape(NZH, 16, 512)
    return pl.pallas_call(
        kernel,
        out_shape=(
            jax.ShapeDtypeStruct((256, DIN), bf16),
            jax.ShapeDtypeStruct((64, 512), f32),
        ),
        in_specs=[pl.BlockSpec(memory_space=pltpu.HBM)] * 3,
        out_specs=(pl.BlockSpec(memory_space=pltpu.VMEM), pl.BlockSpec(memory_space=pltpu.VMEM)),
        scratch_shapes=[
            vmem((256, DIN), bf16),
            vmem((256, 512), bf16),
            vmem((2, NY, 2, NZH, 16, 512), bf16),
            vmem((16, 512), bf16),
            vmem((8, 2, 8, 16, 512), bf16),
            vmem((8, 2, 8, 16, 512), bf16),
            vmem((8, 8, 2, 16, 256), bf16),
            vmem((8, 2, 8, 16, 256), bf16),
            vmem((7, 8, 2, 16, 256), bf16),
            vmem((7, 2, 8, 16, 256), bf16),
            vmem((8, 2, 16, 256), bf16),
            vmem((8, 2, 16, 256), bf16),
            vmem((7, 2, 16, 256), bf16),
            vmem((7, 2, 16, 256), bf16),
            vmem((2, 4, 16, HD), f32),
            vmem((7, 16, HD), f32),
            vmem((8, 16, HD), f32),
            vmem((8, 16, HD), f32),
            vmem((16, HD), f32),
            vmem((16, HD), f32),
            vmem((7, 16, HD), f32),
            vmem((8, 16, HD), f32),
            vmem((4, 64, HD), UPDATE_DTYPE),
            vmem((2, 64, HD), UPDATE_DTYPE),
            dma((6,)), dma, dma((4,)), dma, dma, dma, dma, dma((2,)), dma((2,)), dma, dma,
            *[dma] * 12, *[dma] * 6, dma, dma, dma, pltpu.SemaphoreType.REGULAR,
        ],
        compiler_params=pltpu.CompilerParams(
            collective_id=0, has_side_effects=True, vmem_limit_bytes=VMEM_LIMIT
        ),
        name="whole",
    )(*(pltpu.with_memory_space_constraint(a, pltpu.HBM) for a in args))


def solution(mesh):
    in_specs = (P(("node", "rep"), None), P(("node", "rep"), None), P("node", None))
    out_specs = (P(("node", "rep"), None), P("node", None))
    return jax.shard_map(
        per_device, mesh=mesh, in_specs=in_specs, out_specs=out_specs, check_vma=False
    )
```

time: 358 us -> 74.7 us (0.21)
  waiting for transfers between devices: 254 us -> 0 us
  Pallas kernels: 0 us -> 72.3 us
  blocking collectives: 65.7 us -> 0 us
  matrix products: 14.6 us -> 0 us
  between operations: 13.9 us -> 0.64 us
  other arithmetic: 7.61 us -> 0 us
    all_gather x3 -> x0, waiting for transfers between devices: 253 us -> none  [the longest x2 187 us: gathered_total(): return lax.all_gather(shard, axis).sum(0)]
    pallas_call x0 -> x1, Pallas kernels: none -> 72.3 us  [per_device(): pl.pallas_call(kernel, out_shape=(jax.ShapeDtypeStruct((256, DIN), bf16),...]
    all_to_all x1 -> x0, blocking collectives: 65.7 us -> none  [summed_on_arrival(): lax.all_to_all(pieces, axis, split_axis=0, concat_axis=0, tiled=True)]
    dot_general x22 -> x0, matrix products: 14.6 us -> none  [the longest x1 3.3 us: per_device(): lax.dot_general(cotangent, lax.all_gather(value_weight, 'node', axis=0, t...]
    reduce_sum x4 -> x0, other arithmetic: 7.47 us -> none  [the longest x2 6.39 us: gathered_total(): return lax.all_gather(shard, axis).sum(0)]
  transfers between devices with their start and end apart: 3 -> 0, of which waited for: 3 -> 0; matrix products, arithmetic and copies ran while one was open for 2% -> 0% of each run, Pallas kernels for 0% -> 0%
where the time goes in v2:
time: 74.7 us; the launch traced here: 74.6 us
  Pallas kernels  72.3 us (97%)
  local copies, waits for them, and re-layouts  1.63 us (2%)
    pallas_call x1, Pallas kernels, per_device(): pl.pallas_call(kernel, out_shape=(jax.ShapeDtypeStruct((256, DIN), bf16),...  72.3 us
    unnamed x2, local copies, waits for them, and re-layouts  1.63 us

profile of v2, /device:TPU:1, one launch (start us, length us, event | category | flops | bytes accessed | tf_op | source)
XLA Modules:
  0.0 74.6 jit_solution(9017669536007161263)
XLA Ops:
  0.6 72.3 %whole.1 = (bf16[256,2048]{1,0:T(8,128)(2,1)S(1)}, f32[64,512]{1,0:T(8,128)S(1)}) custom-call(bf16[256,2048]{1,0:T(8,128)(2,1)} %tok_hbm.1, bf16[256,512]{1,0:T(8,128)(2,1)} %cot_hbm.1, bf16[4,16,512]{2,1,0:T(8,128)(2,1)} %bitcast.1), custom_call_target="tpu_custom_call" | custom-call | tf_op jit(solution)/shard_map/whole/pallas_call | solution.py:320
  73.0 1.0 %copy.7 = bf16[256,2048]{1,0:T(8,128)(2,1)} copy(bf16[256,2048]{1,0:T(8,128)(2,1)S(1)} %get-tuple-element.4) | data formatting | bytes 2097152
  73.9 0.7 copy.8

commit v3 on v2

v3 whole, which is shorter than its diff:
```python
import functools
import math

import jax
import jax.numpy as jnp
from jax import lax
from jax.experimental import pallas as pl
from jax.experimental.pallas import tpu as pltpu
from jax.sharding import PartitionSpec as P

MESH = pl.DeviceIdType.MESH

DIN = 2048
HD = 128
NS_ITERS = 5

coef_a = 3.4445
coef_b = -4.775
coef_c = 2.0315
epsilon = 1e-07

NX, NY, NZ, NZH = 8, 8, 8, 4
FAR = (4, 3, 5, 2, 6, 1, 7)
UPDATE_DTYPE = jnp.bfloat16
VMEM_LIMIT = 24 * 1024 * 1024


def split(a):
    parts, rest = [], a
    for _ in range(3):
        parts.append(rest.astype(jnp.bfloat16))
        rest = rest - parts[-1].astype(jnp.float32)
    p, q, r = parts
    left = jnp.concatenate([p, q], axis=1), jnp.concatenate([p, r], axis=1)
    right = (
        jnp.concatenate([jnp.concatenate([p, q], axis=1), jnp.concatenate([q, p], axis=1)], axis=0),
        jnp.concatenate([r, p], axis=0),
    )
    return left, right


def mm(a, b):
    (pq, pr), _ = a
    _, (square, rp) = b
    main = jnp.dot(pq, square, preferred_element_type=jnp.float32)
    return main[:, :HD] + (main[:, HD:] + jnp.dot(pr, rp, preferred_element_type=jnp.float32))


def kernel(
    tok_hbm, cot_hbm, w_hbm, ig_ref, up_ref,
    tok, cot, wfull, wown,
    termx, termy, other, pxa, pxb, pya, pyb, zx, zr, rxa, rxb, ry, sx, sy, r2x, r2y,
    qz, rz, gh, af, rc, bslice, rg, gram, ub, uz,
    load_sem, d2d_s, d2d_r, w0_s, w0_r, w1_s, w1_r, w2_s, w2_r, w3_s, w3_r, zx_s, zx_r,
    x1_s, x1_r, y1a_s, y1b_s, y1_r, x2_s, x2_r, y2_s, y2_r, z_s, z_r, g_s, g_r,
    c_s, c_r, b_s, b_r, a_s, a_r, u_s, v_s, u_r,
):
    node, rep = lax.axis_index("node"), lax.axis_index("rep")
    core = lax.rem(node, 2)
    y = lax.rem(lax.div(node, 2), NY)
    zl = lax.div(node, 2 * NY)
    x, zh = lax.div(rep, NZH), lax.rem(rep, NZH)
    z = zh * 2 + zl

    def dev(x_=None, y_=None, z_=None, core_=None):
        to = {}
        if y_ is not None or z_ is not None or core_ is not None:
            low = zl if z_ is None else lax.rem(z_, 2)
            to["node"] = (low * NY + (y if y_ is None else y_)) * 2 + (core if core_ is None else core_)
        if x_ is not None or z_ is not None:
            to["rep"] = (x if x_ is None else x_) * NZH + (zh if z_ is None else lax.div(z_, 2))
        return to

    def ahead(at, d, n):
        return lax.rem(at + d, n)

    def describe(src, dst, ssem, rsem, to):
        return pltpu.make_async_remote_copy(
            src_ref=src, dst_ref=dst, send_sem=ssem, recv_sem=rsem, device_id=to, device_id_type=MESH
        )

    def send(src, dst, ssem, rsem, to):
        describe(src, dst, ssem, rsem, to).start()

    def wait(like, sem):
        pltpu.make_async_copy(like, like, sem).wait()

    partner = dev(core_=1 - core)

    load_cot = pltpu.make_async_copy(cot_hbm, cot, load_sem.at[0])
    load_cot.start()
    pairs = [lax.rem(lax.div(y, 2) + 2 + k, 4) for k in range(4)]
    for k in range(4):
        for lo in range(2):
            columns = pl.ds(pl.multiple_of(lo * 1024 + pairs[k] * 256, 256), 256)
            slot = pl.ds(lo * 1024 + k * 256, 256)
            pltpu.make_async_copy(tok_hbm.at[:, columns], tok.at[:, slot], load_sem.at[2 + k]).start()
    load_w = pltpu.make_async_copy(w_hbm.at[zh], wown, load_sem.at[1])
    load_w.start()

    barrier = pltpu.get_barrier_semaphore()

    def greet(to):
        pl.semaphore_signal(barrier, inc=1, device_id=to, device_id_type=MESH)

    def z_hi_peer(d, core_):
        return dev(z_=lax.rem(zh + d, NZH) * 2 + zl, core_=core_)

    for d in FAR:
        greet(dev(z_=ahead(z, d, NZ)))
        greet(dev(y_=ahead(y, d, NY)))
        greet(dev(y_=ahead(y, d, NY), core_=1 - core))

        @pl.when(core == 1)
        def _(d=d):
            greet(dev(x_=ahead(x, d, NX)))

        if d == 4:

            @pl.when(core == 0)
            def _():
                for e in (2, 1, 3):
                    greet(z_hi_peer(e, 1))

    greet(partner)

    def compute(k):
        wait(tok.at[:, pl.ds(0, 512)], load_sem.at[2 + k])
        for lo in range(2):
            t = lax.dot_general(
                tok[:, lo * 1024 + k * 256 : lo * 1024 + k * 256 + 256],
                cot[...],
                (((0,), (0,)), ((), ())),
                preferred_element_type=jnp.float32,
            )
            t = t.reshape(2, 8, 16, 512).astype(jnp.bfloat16)
            termx[2 * k : 2 * k + 2, lo] = t[..., :256]
            termy[2 * k : 2 * k + 2, lo] = t[..., 256:]

    def summed(term, b, lo):
        return term[b, lo] + other[b, lo]

    pair = dev(z_=z + 1 - 2 * zl)

    def piece(at):
        return wfull.at[lax.rem(at, 2), :, :, lax.div(at, 2)]

    def finish():
        for k in range(8):
            lo, b = k // 4, 2 * (k % 4)
            weight = wfull[lo, b : b + 2].reshape(256, 512)
            ig_ref[:, k * 256 : k * 256 + 256] = lax.dot_general(
                cot[...], weight, (((1,), (1,)), ((), ())), preferred_element_type=jnp.float32
            ).astype(jnp.bfloat16)

    def place():
        for h in range(4):
            up_ref[:, h * HD : h * HD + HD] = ub[h].astype(jnp.float32)

    to_partner = describe(wown, wfull.at[zl, y, 1, zh], w0_s, w0_r, partner)

    @pl.when(core == 0)
    def _():
        load_cot.wait()
        for k in range(4):
            compute(k)
            if k == 0:
                pl.semaphore_wait(barrier, 22)
            ys = pl.ds(2 * k, 2)
            send(termx.at[ys], other.at[ys], d2d_s, d2d_r.at[k], partner)
            if k == 0:
                load_w.wait()
                for d in FAR:
                    send(wown, wfull.at[zl, y, 0, zh], w1_s, w1_r, dev(y_=ahead(y, d, NY)))
        wfull[zl, y, 0, zh] = wown[...]

        for k in range(4):
            wait(other.at[pl.ds(2 * k, 2)], d2d_r.at[k])
            zx[k] = summed(termy, 2 * k + 1, 1 - zl)
            send(zx.at[k], zr.at[k], zx_s, zx_r.at[k], pair)
            for lo in range(2):
                pya[k, lo] = summed(termy, 2 * k, lo)
            at_y = 2 * pairs[k]
            send(pya.at[k], ry.at[lax.rem(at_y + NY + 7 - y, NY)], y1a_s, y1_r, dev(y_=at_y, core_=1))
            pyb[k] = summed(termy, 2 * k + 1, zl)
        sevenths = wfull.at[0, pl.ds(0, 7), :, 0]

        def hop(at, up, step):
            to_z = ahead(z, 1 if up else NZ - 1, NZ)
            k = 2 * step + (0 if up else 1)
            send(piece(at), piece(at), w2_s.at[0 if up else 1], w2_r.at[k], dev(z_=to_z))

        for k in range(4):
            if k == 2:
                to_partner.wait_recv()
                wait(sevenths, w1_r)
                hop(z, True, 0)
                hop(z, False, 0)
                send(piece(z), piece(z), w3_s, w3_r, partner)
            wait(zr.at[k], zx_r.at[k])
            pyb[k] = pyb[k] + zr[k]
            at_y = 2 * pairs[k] + 1
            send(pyb.at[k], ry.at[lax.rem(at_y + NY + 7 - y, NY), 0], y1b_s, y1_r, dev(y_=at_y, core_=1))

        for step in range(4):
            for up in (True, False) if step < 3 else (True,):
                at = lax.rem(z + (NZ - 1 - step if up else 1 + step), NZ)
                wait(piece(at), w2_r.at[2 * step + (0 if up else 1)])
                if step < (3 if up else 2):
                    hop(at, up, step + 1)
                send(piece(at), piece(at), w3_s, w3_r, partner)
        finish()
        wait(termx, d2d_s)
        wait(zx, zx_s)
        wait(pya, y1a_s)
        wait(pyb, y1b_s)
        wait(wfull.at[0, pl.ds(0, 7), 0, 0], w1_s)
        wait(wfull.at[0], w2_s.at[0])
        wait(wfull.at[0, :, :, pl.ds(0, 3)], w2_s.at[1])
        wait(wfull, w3_s)
        wait(ub, u_r)
        place()

    @pl.when(core == 1)
    def _():
        load_cot.wait()
        for k in range(4):
            compute(k)
            if k == 0:
                pl.semaphore_wait(barrier, 32)
            ys = pl.ds(2 * k, 2)
            send(termy.at[ys], other.at[ys], d2d_s, d2d_r.at[k], partner)
            if k == 0:
                load_w.wait()
                to_partner.start()
                for d in FAR:
                    send(wown, wfull.at[zl, y, 1, zh], w1_s, w1_r, dev(y_=ahead(y, d, NY), core_=0))

        for k in range(4):
            wait(other.at[pl.ds(2 * k, 2)], d2d_r.at[k])
            zx[k] = summed(termx, 2 * k + 1, 1 - zl)
            send(zx.at[k], zr.at[k], zx_s, zx_r.at[k], pair)
            for lo in range(2):
                pxa[:, k, lo] = summed(termx, 2 * k, lo)
            pxb[:, k] = summed(termx, 2 * k + 1, zl)
            if k % 2 == 1:
                ks = pl.ds(k - 1, 2)
                for d in FAR:
                    to_x = ahead(x, d, NX)
                    send(pxa.at[to_x, ks], rxa.at[d - 1, ks], x1_s.at[0], x1_r.at[0], dev(x_=to_x))
        for k in range(4):
            wait(zr.at[k], zx_r.at[k])
            pxb[:, k] = pxb[:, k] + zr[k]
            if k % 2 == 1:
                ks = pl.ds(k - 1, 2)
                for d in FAR:
                    to_x = ahead(x, d, NX)
                    send(pxb.at[to_x, ks], rxb.at[d - 1, ks], x1_s.at[1], x1_r.at[1], dev(x_=to_x))

        def total_of(first, parts):
            total = first.astype(jnp.float32)
            for part in parts:
                total += part.astype(jnp.float32)
            return total

        def middle(odd):
            n = 1 if odd else 2
            wait(rxa, x1_r.at[0])
            for k in range(4):
                for lo in range(2):
                    total = total_of(pxa[x, k, lo], [rxa[i, k, lo] for i in range(7)])
                    sx[2 * pairs[k], lo] = total.astype(jnp.bfloat16)
            wait(rxb, x1_r.at[1])
            for k in range(4):
                total = total_of(pxb[x, k], [rxb[i, k] for i in range(7)])
                sx[2 * pairs[k] + 1, 0] = total.astype(jnp.bfloat16)
            for d in FAR:
                to_y, m = ahead(y, d, NY), 1 if (d + odd) % 2 else 2
                part = pl.ds(0, m)
                send(sx.at[to_y, part], r2x.at[d - 1, part], y2_s.at[d % 2], y2_r, dev(y_=to_y))
            wait(ry.at[:, pl.ds(0, n)], y1_r)
            for b in range(8):
                for lo in range(n):
                    total = total_of(ry[7, lo, b], [ry[i, lo, b] for i in range(7)])
                    sy[b, lo] = total.astype(jnp.bfloat16)
            part = pl.ds(0, n)
            for d in FAR:
                to_x = ahead(x, d, NX)
                send(sy.at[to_x, part], r2y.at[d - 1, part], x2_s, x2_r, dev(x_=to_x))
            wait(r2x.at[:, part], y2_r)
            wait(r2y.at[:, part], x2_r)
            for lo in range(n):
                total_x = total_of(sx[y, lo], [r2x[i, lo] for i in range(7)])
                total_y = total_of(sy[x, lo], [r2y[i, lo] for i in range(7)])
                for h in range(4):
                    source = total_x if h < 2 else total_y
                    qz[lo, h] = source[:, (h % 2) * HD : (h % 2) * HD + HD]
            if odd:
                for d in (2, 1, 3):
                    to_h = lax.rem(zh + d, NZH)
                    send(qz.at[0, to_h], rz.at[d - 1], z_s, z_r, z_hi_peer(d, 1))
                slots = 3
            else:
                for d in FAR:
                    to_z = ahead(z, d, NZ)
                    send(qz.at[lax.rem(to_z, 2), lax.div(to_z, 2)], rz.at[d - 1], z_s, z_r, dev(z_=to_z))
                slots = 7
            wait(rz.at[pl.ds(0, slots)], z_r)
            rows = qz[0 if odd else zl, zh]
            for i in range(slots):
                rows += rz[i]
            gh[x] = rows
            wait(r2x.at[pl.ds(0, 4), pl.ds(0, 2 if odd else 1)], y2_s.at[1])
            wait(r2x.at[pl.ds(0, 3), pl.ds(0, 1 if odd else 2)], y2_s.at[0])
            wait(r2y.at[:, part], x2_s)
            wait(rz.at[pl.ds(0, slots)], z_s)

        odd_y = lax.rem(y, 2)

        @pl.when(odd_y == 0)
        def _():
            middle(0)

        @pl.when(odd_y == 1)
        def _():
            middle(1)

        for d in FAR:
            send(gh.at[x], gh.at[x], g_s, g_r, dev(x_=ahead(x, d, NX)))
        others = gh.at[pl.ds(0, 7)]
        wait(others, g_r)

        g = gh[...].reshape(128, HD)
        partial = lax.dot_general(
            g, g, (((0,), (0,)), ((), ())), precision=lax.Precision.HIGHEST, preferred_element_type=jnp.float32
        )
        af[...] = partial.reshape(8, 16, HD)

        send(af.at[x], rc, c_s, c_r, pair)
        wait(rc, c_r)
        bslice[...] = af[x] + rc[...]

        for d in FAR:
            send(bslice, rg.at[d - 1], b_s, b_r, dev(y_=ahead(y, d, NY)))
        wait(rg, b_r)
        total = bslice[...]
        for i in range(7):
            total += rg[i]
        gram[x] = total

        for d in FAR:
            send(gram.at[x], gram.at[x], a_s, a_r, dev(x_=ahead(x, d, NX)))
        wait(others, a_r)

        a = gram[...].reshape(HD, HD)
        row = lax.broadcasted_iota(jnp.int32, (HD, HD), 0)
        col = lax.broadcasted_iota(jnp.int32, (HD, HD), 1)
        eye = row == col
        identity = jnp.where(eye, 1.0, 0.0).astype(jnp.float32)
        square = jnp.sum(jnp.where(eye, a, 0.0), axis=0, keepdims=True)
        square = jnp.sum(square, axis=1, keepdims=True)
        divisor = jnp.sqrt(square) + epsilon
        a = a / (divisor * divisor)
        total = None
        for step in range(NS_ITERS):
            parts = split(a)
            factor = coef_a * identity + coef_b * a + coef_c * mm(parts, parts)
            f = split(factor)
            total = factor if total is None else mm(split(total), f)
            if step + 1 < NS_ITERS:
                a = mm(f, split(mm(parts, f)))
        result = (0.2 * math.sqrt(DIN)) * mm(split(gh[...].reshape(128, HD) / divisor), split(total))
        result = result.astype(uz.dtype).reshape(2, 64, HD)
        uz[...] = result
        ub[zh] = result[1]

        for d in (2, 1, 3):
            send(uz.at[1], ub.at[zh], u_s, u_r, z_hi_peer(d, 1))
            send(uz.at[0], ub.at[zh], v_s, u_r, z_hi_peer(d, 0))
        send(uz.at[0], ub.at[zh], v_s, u_r, partner)

        wait(wfull, w3_r)
        finish()
        to_partner.wait_send()
        for like, sem in (
            (termy, d2d_s), (zx, zx_s), (wfull.at[0, pl.ds(0, 7), 0, 0], w1_s),
            (rxa, x1_s.at[0]), (rxb, x1_s.at[1]),
            (others, g_s), (rc, c_s), (rg, b_s), (others, a_s),
        ):
            wait(like, sem)
        three = ub.at[pl.ds(0, 3)]
        wait(three, u_r)
        place()
        wait(three, u_s)
        wait(ub, v_s)


def store(ig_ref, up_ref, ig_hbm, up_hbm, sems):
    copies = [
        pltpu.make_async_copy(ig_ref.at[pl.ds(64 * k, 64)], ig_hbm.at[pl.ds(64 * k, 64)], sems.at[k]) for k in range(4)
    ]
    copies.append(pltpu.make_async_copy(up_ref, up_hbm, sems.at[4]))
    for copy in copies:
        copy.start()
    for copy in copies:
        copy.wait()


def per_device(tokens, cotangent, value_weight):
    bf16, f32 = jnp.bfloat16, jnp.float32
    vmem, dma = pltpu.VMEM, pltpu.SemaphoreType.DMA
    args = tokens, cotangent, value_weight.reshape(NZH, 16, 512)
    results = pl.pallas_call(
        kernel,
        out_shape=(
            jax.ShapeDtypeStruct((256, DIN), bf16),
            jax.ShapeDtypeStruct((64, 512), f32),
        ),
        in_specs=[pl.BlockSpec(memory_space=pltpu.HBM)] * 3,
        out_specs=(pl.BlockSpec(memory_space=pltpu.VMEM), pl.BlockSpec(memory_space=pltpu.VMEM)),
        scratch_shapes=[
            vmem((256, DIN), bf16),
            vmem((256, 512), bf16),
            vmem((2, NY, 2, NZH, 16, 512), bf16),
            vmem((16, 512), bf16),
            vmem((8, 2, 8, 16, 256), bf16),
            vmem((8, 2, 8, 16, 256), bf16),
            vmem((8, 2, 8, 16, 256), bf16),
            vmem((8, 4, 2, 16, 256), bf16),
            vmem((8, 4, 16, 256), bf16),
            vmem((4, 2, 8, 16, 256), bf16),
            vmem((4, 8, 16, 256), bf16),
            vmem((4, 8, 16, 256), bf16),
            vmem((4, 8, 16, 256), bf16),
            vmem((7, 4, 2, 16, 256), bf16),
            vmem((7, 4, 16, 256), bf16),
            vmem((8, 2, 8, 16, 256), bf16),
            vmem((8, 2, 16, 256), bf16),
            vmem((8, 2, 16, 256), bf16),
            vmem((7, 2, 16, 256), bf16),
            vmem((7, 2, 16, 256), bf16),
            vmem((2, 4, 16, HD), f32),
            vmem((7, 16, HD), f32),
            vmem((8, 16, HD), f32),
            vmem((8, 16, HD), f32),
            vmem((16, HD), f32),
            vmem((16, HD), f32),
            vmem((7, 16, HD), f32),
            vmem((8, 16, HD), f32),
            vmem((4, 64, HD), UPDATE_DTYPE),
            vmem((2, 64, HD), UPDATE_DTYPE),
            dma((6,)), dma, dma((4,)), dma, dma, dma, dma, dma((2,)), dma((7,)), dma, dma, dma, dma((4,)),
            dma((2,)), dma((2,)), dma, dma, dma, dma, dma, dma((2,)), dma, *[dma] * 4,
            *[dma] * 6, dma, dma, dma,
        ],
        compiler_params=pltpu.CompilerParams(
            collective_id=0, has_side_effects=True, vmem_limit_bytes=VMEM_LIMIT
        ),
        name="whole",
    )(*(pltpu.with_memory_space_constraint(a, pltpu.HBM) for a in args))
    return pl.pallas_call(
        store,
        out_shape=(
            jax.ShapeDtypeStruct((256, DIN), bf16),
            jax.ShapeDtypeStruct((64, 512), f32),
        ),
        in_specs=[pl.BlockSpec(memory_space=pltpu.VMEM)] * 2,
        out_specs=(pl.BlockSpec(memory_space=pltpu.HBM), pl.BlockSpec(memory_space=pltpu.HBM)),
        scratch_shapes=[dma((5,))],
        compiler_params=pltpu.CompilerParams(vmem_limit_bytes=8 * 1024 * 1024),
        name="store",
    )(*results)


def solution(mesh):
    in_specs = (P(("node", "rep"), None), P(("node", "rep"), None), P("node", None))
    out_specs = (P(("node", "rep"), None), P("node", None))
    return jax.shard_map(
        per_device, mesh=mesh, in_specs=in_specs, out_specs=out_specs, check_vma=False
    )
```

time: 74.7 us -> 69.1 us (0.925)
  Pallas kernels: 72.3 us -> 68.3 us
  local copies, waits for them, and re-layouts: 1.63 us -> 0 us
    pallas_call x1, Pallas kernels: 72.3 us -> 67.3 us  [per_device(): pl.pallas_call(kernel, out_shape=(jax.ShapeDtypeStruct((256, DIN), bf16),...]
    unnamed x2 -> x0, local copies, waits for them, and re-layouts: 1.63 us -> none
    pallas_call x0 -> x1, Pallas kernels: none -> 1.05 us  [per_device(): pl.pallas_call(store, out_shape=(jax.ShapeDtypeStruct((256, DIN), bf16),...]
where the time goes in v3:
time: 69.1 us; the launch traced here: 68.9 us
  Pallas kernels  68.3 us (99%)
    pallas_call x1, Pallas kernels, per_device(): pl.pallas_call(kernel, out_shape=(jax.ShapeDtypeStruct((256, DIN), bf16),...  67.3 us

profile of v3, /device:TPU:1, one launch (start us, length us, event | category | flops | bytes accessed | tf_op | source)
XLA Modules:
  0.0 68.9 jit_solution(600808326391114496)
XLA Ops:
  0.6 67.3 %whole.1 = (bf16[256,2048]{1,0:T(8,128)(2,1)S(1)}, f32[64,512]{1,0:T(8,128)S(1)}) custom-call(bf16[256,2048]{1,0:T(8,128)(2,1)} %tok_hbm.1, bf16[256,512]{1,0:T(8,128)(2,1)} %cot_hbm.1, bf16[4,16,512]{2,1,0:T(8,128)(2,1)} %bitcast.1), custom_call_target="tpu_custom_call" | custom-call | tf_op jit(solution)/shard_map/whole/pallas_call | solution.py:413
  67.9 1.0 %store.1 = (bf16[256,2048]{1,0:T(8,128)(2,1)}, f32[64,512]{1,0:T(8,128)}) custom-call(bf16[256,2048]{1,0:T(8,128)(2,1)S(1)} %get-tuple-element.4.ig_ref, f32[64,512]{1,0:T(8,128)S(1)} %get-tuple-element.5.up_ref), custom_call_target="tpu_custom_call" | custom-call | tf_op jit(solution)/shard_map/store/pallas_call | solution.py:461

commit v4 on v3

--- a/solution.py
+++ b/solution.py
@@ -49,11 +49,11 @@
 def kernel(
     tok_hbm, cot_hbm, w_hbm, ig_ref, up_ref,
     tok, cot, wfull, wown,
-    termx, termy, other, pxa, pxb, pya, pyb, zx, zr, rxa, rxb, ry, sx, sy, r2x, r2y,
-    qz, rz, gh, af, rc, bslice, rg, gram, ub, uz,
-    load_sem, d2d_s, d2d_r, w0_s, w0_r, w1_s, w1_r, w2_s, w2_r, w3_s, w3_r, zx_s, zx_r,
+    termx, termy, other, pxa, pxb, pya, pyb, zx, zr, fxa, fya, rxa, rxb, ry, sx, sy, r2x, r2y,
+    qz, rz, gh, af, rg, gram, ub, uz,
+    load_sem, d2d_s, d2d_r, w0_s, w0_r, w1_s, w1_r, w2_s, w2_r, w3_s, w3_r, zx_s, zx_r, f_s, f_r,
     x1_s, x1_r, y1a_s, y1b_s, y1_r, x2_s, x2_r, y2_s, y2_r, z_s, z_r, g_s, g_r,
-    c_s, c_r, b_s, b_r, a_s, a_r, u_s, v_s, u_r,
+    b_s, b_r, a_s, a_r, u_s, v_s, u_r,
 ):
     node, rep = lax.axis_index("node"), lax.axis_index("rep")
     core = lax.rem(node, 2)
@@ -114,13 +114,6 @@
         @pl.when(core == 1)
         def _(d=d):
             greet(dev(x_=ahead(x, d, NX)))
-
-        if d == 4:
-
-            @pl.when(core == 0)
-            def _():
-                for e in (2, 1, 3):
-                    greet(z_hi_peer(e, 1))
 
     greet(partner)
 
@@ -158,6 +151,21 @@
             up_ref[:, h * HD : h * HD + HD] = ub[h].astype(jnp.float32)
 
     to_partner = describe(wown, wfull.at[zl, y, 1, zh], w0_s, w0_r, partner)
+
+    odd_y = lax.rem(y, 2)
+
+    def whole_rows(k, odd):
+        d = ((4, 6, 0, 2), (3, 5, 7, 1))[odd][k]
+
+        @pl.when(odd_y == odd)
+        def _():
+            if d == 4:
+                send(pya.at[k], fya, f_s.at[1], f_r.at[2], dev(y_=ahead(y, NY - 1, NY)))
+            elif d != 5:
+                send(pya.at[k], ry.at[(d + 7) % 8], y1a_s, y1_r, dev(y_=2 * pairs[k], core_=1))
+
+    behind = dev(x_=ahead(x, NX - 1, NX))
+    x5 = ahead(x, 5, NX)
 
     @pl.when(core == 0)
     def _():
@@ -180,8 +188,8 @@
             send(zx.at[k], zr.at[k], zx_s, zx_r.at[k], pair)
             for lo in range(2):
                 pya[k, lo] = summed(termy, 2 * k, lo)
-            at_y = 2 * pairs[k]
-            send(pya.at[k], ry.at[lax.rem(at_y + NY + 7 - y, NY)], y1a_s, y1_r, dev(y_=at_y, core_=1))
+            whole_rows(k, 0)
+            whole_rows(k, 1)
             pyb[k] = summed(termy, 2 * k + 1, zl)
         sevenths = wfull.at[0, pl.ds(0, 7), :, 0]
 
@@ -201,6 +209,13 @@
             pyb[k] = pyb[k] + zr[k]
             at_y = 2 * pairs[k] + 1
             send(pyb.at[k], ry.at[lax.rem(at_y + NY + 7 - y, NY), 0], y1b_s, y1_r, dev(y_=at_y, core_=1))
+            if k == 1:
+
+                @pl.when(odd_y == 1)
+                def _():
+                    wait(fya, f_r.at[2])
+                    pya[1] = pya[1] + fya[...]
+                    send(pya.at[1], ry.at[4], y1a_s, y1_r, dev(y_=2 * pairs[1], core_=1))
 
         for step in range(4):
             for up in (True, False) if step < 3 else (True,):
@@ -212,7 +227,16 @@
         finish()
         wait(termx, d2d_s)
         wait(zx, zx_s)
-        wait(pya, y1a_s)
+
+        @pl.when(odd_y == 0)
+        def _():
+            wait(pya.at[pl.ds(0, 3)], y1a_s)
+            wait(fya, f_s.at[1])
+
+        @pl.when(odd_y == 1)
+        def _():
+            wait(pya, y1a_s)
+
         wait(pyb, y1b_s)
         wait(wfull.at[0, pl.ds(0, 7), 0, 0], w1_s)
         wait(wfull.at[0], w2_s.at[0])
@@ -227,7 +251,7 @@
         for k in range(4):
             compute(k)
             if k == 0:
-                pl.semaphore_wait(barrier, 32)
+                pl.semaphore_wait(barrier, 29)
             ys = pl.ds(2 * k, 2)
             send(termy.at[ys], other.at[ys], d2d_s, d2d_r.at[k], partner)
             if k == 0:
@@ -245,14 +269,21 @@
             pxb[:, k] = summed(termx, 2 * k + 1, zl)
             if k % 2 == 1:
                 ks = pl.ds(k - 1, 2)
-                for d in FAR:
-                    to_x = ahead(x, d, NX)
-                    send(pxa.at[to_x, ks], rxa.at[d - 1, ks], x1_s.at[0], x1_r.at[0], dev(x_=to_x))
+                send(pxa.at[ahead(x, 4, NX), ks], fxa.at[ks], f_s.at[0], f_r.at[k // 2], behind)
+                for d in (3, 2, 6, 1, 7):
+                    to_x, at = ahead(x, d, NX), d - 1 if d < 4 else d - 2
+                    send(pxa.at[to_x, ks], rxa.at[at, ks], x1_s.at[0], x1_r.at[0], dev(x_=to_x))
         for k in range(4):
             wait(zr.at[k], zx_r.at[k])
             pxb[:, k] = pxb[:, k] + zr[k]
-            if k % 2 == 1:
-                ks = pl.ds(k - 1, 2)
+            if k == 0:
+                for j in range(2):
+                    ks = pl.ds(2 * j, 2)
+                    wait(fxa.at[ks], f_r.at[j])
+                    pxa[x5, 2 * j : 2 * j + 2] = pxa[x5, 2 * j : 2 * j + 2] + fxa[2 * j : 2 * j + 2]
+                    send(pxa.at[x5, ks], rxa.at[3, ks], x1_s.at[0], x1_r.at[0], dev(x_=x5))
+            if k >= 1:
+                ks = pl.ds(0, 2) if k == 1 else pl.ds(k, 1)
                 for d in FAR:
                     to_x = ahead(x, d, NX)
                     send(pxb.at[to_x, ks], rxb.at[d - 1, ks], x1_s.at[1], x1_r.at[1], dev(x_=to_x))
@@ -268,7 +299,7 @@
             wait(rxa, x1_r.at[0])
             for k in range(4):
                 for lo in range(2):
-                    total = total_of(pxa[x, k, lo], [rxa[i, k, lo] for i in range(7)])
+                    total = total_of(pxa[x, k, lo], [rxa[i, k, lo] for i in range(6)])
                     sx[2 * pairs[k], lo] = total.astype(jnp.bfloat16)
             wait(rxb, x1_r.at[1])
             for k in range(4):
@@ -278,10 +309,10 @@
                 to_y, m = ahead(y, d, NY), 1 if (d + odd) % 2 else 2
                 part = pl.ds(0, m)
                 send(sx.at[to_y, part], r2x.at[d - 1, part], y2_s.at[d % 2], y2_r, dev(y_=to_y))
-            wait(ry.at[:, pl.ds(0, n)], y1_r)
+            wait(ry.at[:, pl.ds(0, 1)] if odd else ry.at[pl.ds(0, 7)], y1_r)
             for b in range(8):
                 for lo in range(n):
-                    total = total_of(ry[7, lo, b], [ry[i, lo, b] for i in range(7)])
+                    total = total_of(ry[7, lo, b], [ry[i, lo, b] for i in range(7) if odd or i != 3])
                     sy[b, lo] = total.astype(jnp.bfloat16)
             part = pl.ds(0, n)
             for d in FAR:
@@ -315,8 +346,6 @@
             wait(r2y.at[:, part], x2_s)
             wait(rz.at[pl.ds(0, slots)], z_s)
 
-        odd_y = lax.rem(y, 2)
-
         @pl.when(odd_y == 0)
         def _():
             middle(0)
@@ -336,15 +365,13 @@
         )
         af[...] = partial.reshape(8, 16, HD)
 
-        send(af.at[x], rc, c_s, c_r, pair)
-        wait(rc, c_r)
-        bslice[...] = af[x] + rc[...]
-
         for d in FAR:
-            send(bslice, rg.at[d - 1], b_s, b_r, dev(y_=ahead(y, d, NY)))
+            send(af.at[x], rg.at[d + 7], b_s, b_r, dev(y_=ahead(y, d, NY), z_=z + 1 - 2 * zl))
+            send(af.at[x], rg.at[d - 1], b_s, b_r, dev(y_=ahead(y, d, NY)))
+        send(af.at[x], rg.at[7], b_s, b_r, pair)
         wait(rg, b_r)
-        total = bslice[...]
-        for i in range(7):
+        total = af[x]
+        for i in range(15):
             total += rg[i]
         gram[x] = total
 
@@ -384,8 +411,8 @@
         to_partner.wait_send()
         for like, sem in (
             (termy, d2d_s), (zx, zx_s), (wfull.at[0, pl.ds(0, 7), 0, 0], w1_s),
-            (rxa, x1_s.at[0]), (rxb, x1_s.at[1]),
-            (others, g_s), (rc, c_s), (rg, b_s), (others, a_s),
+            (rxa, x1_s.at[0]), (fxa, f_s.at[0]), (rxb, x1_s.at[1]),
+            (others, g_s), (rg, b_s), (others, a_s),
         ):
             wait(like, sem)
         three = ub.at[pl.ds(0, 3)]
@@ -432,7 +459,9 @@
             vmem((4, 8, 16, 256), bf16),
             vmem((4, 8, 16, 256), bf16),
             vmem((4, 8, 16, 256), bf16),
-            vmem((7, 4, 2, 16, 256), bf16),
+            vmem((4, 2, 16, 256), bf16),
+            vmem((2, 8, 16, 256), bf16),
+            vmem((6, 4, 2, 16, 256), bf16),
             vmem((7, 4, 16, 256), bf16),
             vmem((8, 2, 8, 16, 256), bf16),
             vmem((8, 2, 16, 256), bf16),
@@ -443,15 +472,13 @@
             vmem((7, 16, HD), f32),
             vmem((8, 16, HD), f32),
             vmem((8, 16, HD), f32),
-            vmem((16, HD), f32),
-            vmem((16, HD), f32),
-            vmem((7, 16, HD), f32),
+            vmem((15, 16, HD), f32),
             vmem((8, 16, HD), f32),
             vmem((4, 64, HD), UPDATE_DTYPE),
             vmem((2, 64, HD), UPDATE_DTYPE),
-            dma((6,)), dma, dma((4,)), dma, dma, dma, dma, dma((2,)), dma((7,)), dma, dma, dma, dma((4,)),
+            dma((6,)), dma, dma((4,)), dma, dma, dma, dma, dma((2,)), dma((7,)), dma, dma, dma, dma((4,)), dma((2,)), dma((3,)),
             dma((2,)), dma((2,)), dma, dma, dma, dma, dma, dma((2,)), dma, *[dma] * 4,
-            *[dma] * 6, dma, dma, dma,
+            *[dma] * 4, dma, dma, dma,
         ],
         compiler_params=pltpu.CompilerParams(
             collective_id=0, has_side_effects=True, vmem_limit_bytes=VMEM_LIMIT

time: 69.1 us -> 66.7 us (0.965)
  Pallas kernels: 68.3 us -> 65.9 us
    pallas_call x1, Pallas kernels: 67.3 us -> 64.9 us  [per_device(): pl.pallas_call(kernel, out_shape=(jax.ShapeDtypeStruct((256, DIN), bf16),...]
where the time goes in v4:
time: 66.7 us; the launch traced here: 66.5 us
  Pallas kernels  65.9 us (99%)
    pallas_call x1, Pallas kernels, per_device(): pl.pallas_call(kernel, out_shape=(jax.ShapeDtypeStruct((256, DIN), bf16),...  64.9 us

profile of v4, /device:TPU:1, one launch (start us, length us, event | category | flops | bytes accessed | tf_op | source)
XLA Modules:
  0.0 66.5 jit_solution(15933879492574146774)
XLA Ops:
  0.6 64.9 %whole.1 = (bf16[256,2048]{1,0:T(8,128)(2,1)S(1)}, f32[64,512]{1,0:T(8,128)S(1)}) custom-call(bf16[256,2048]{1,0:T(8,128)(2,1)} %tok_hbm.1, bf16[256,512]{1,0:T(8,128)(2,1)} %cot_hbm.1, bf16[4,16,512]{2,1,0:T(8,128)(2,1)} %bitcast.1), custom_call_target="tpu_custom_call" | custom-call | tf_op jit(solution)/shard_map/whole/pallas_call | solution.py:440
  65.5 1.0 %store.1 = (bf16[256,2048]{1,0:T(8,128)(2,1)}, f32[64,512]{1,0:T(8,128)}) custom-call(bf16[256,2048]{1,0:T(8,128)(2,1)S(1)} %get-tuple-element.4.ig_ref, f32[64,512]{1,0:T(8,128)S(1)} %get-tuple-element.5.up_ref), custom_call_target="tpu_custom_call" | custom-call | tf_op jit(solution)/shard_map/store/pallas_call | solution.py:488
